TPU v7x, 256 devices: a 4x2x16 block of a 4x16x16 slice. The times are simulated.
256 devices in a mesh: groups: 2 (over y), dp: 32 (over z, core), expert: 4 (over x).
Axes of the slice: x: 4, y: 2, z: 16, core: 2. Of those that a mesh axis runs over, the one named last changes fastest.
The devices are a block of a 4x16x16 slice.
Arguments:
- queries: bfloat16 [2, 1024, 32, 128], P(None, ('groups', 'dp'), 'expert'), parts along dimension 1, may hold values from -6 to 6
- fresh_kv: bfloat16 [2, 1024, 4, 256], P(None, ('groups', 'dp'), 'expert'), parts along dimension 1, may hold values from -6 to 6
- kv_pool: bfloat16 [20480, 16, 4, 256], P(('groups', 'dp'), None, 'expert'), parts along dimension 0, may hold values from -6 to 6
- page_table: int32 [1024, 305], P(('groups', 'dp')), parts along dimension 0, may hold values from -1 to 319, as said below
- context_lengths: int32 [1024], P(('groups', 'dp')), parts along dimension 0, may hold values from 1 to 4880, as said below
- residual: bfloat16 [2, 1024, 4096], P(None, ('groups', 'dp'), 'expert'), parts along dimension 1, may hold values from -16 to 16
- out_weight: bfloat16 [4096, 4096], P('expert', 'dp'), may hold values from -0.09375 to 0.09375
- norm_gain: float32 [4096], P('expert'), may hold values from 0.1 to 1.9
- expert_ids: int32 [2, 1024, 8], P(None, ('groups', 'dp')), parts along dimension 1, may hold values from 0 to 63, all different within a row; in each aligned block of 16 rows (0 to 15, 16 to 31, ..., all dimensions but the last counted through in order) at most 5 rows name the same one
- route_weights: float32 [2, 1024, 8], P(None, ('groups', 'dp')), parts along dimension 1, may hold values from 0.1 to 1
- gate_up: bfloat16 [64, 2, 4096, 768], P('dp', None, 'expert'), may hold values from -0.09375 to 0.09375
- down_proj: bfloat16 [64, 768, 4096], P('dp', None, 'expert'), may hold values from -0.21875 to 0.21875
Outputs:
- layer_out: bfloat16 [2, 1024, 4096], P(None, ('groups', 'dp'), 'expert'), parts along dimension 1
There are 2 independent parts, one for each index of `groups`. A program takes and returns all parts, laid end to end along the dimension named above; an argument that names none is the same for every part. Nothing has to cross between parts.
Inputs may be any that keep to these rules, and one draw needn't show every extreme that they name: `page_table`: entries 0 to ceil(context_lengths[i] / 16) - 1 of a row name distinct pages, no page is named twice within the 16 requests of one block, and later entries are -1. The requests of one block hold at most 320 pages together; in every draw some block holds exactly 320, and some request holds exactly 305 pages. `context_lengths`: every request holds at least one cached token; in every draw some request holds exactly 4880. `expert_ids`: within the rows of one device (16 requests of one step) no expert is named by more than 5 rows.
All inputs are finite; a program needn't handle non-finite values.
Results may differ from a plain program's by a relative error of at most 0.005.
Values may be sent and summed in bfloat16 or wider, within the bound.
A program may use at most 64 MiB of HBM per device.

v0:
```python
import math

import jax
import jax.numpy as jnp
from jax import lax
from jax.sharding import PartitionSpec as P

NEG = -1e30
EPS = 1e-06
EXACT = lax.Precision.HIGHEST


def in_blocks(array, dim, length):
    before, after = (array.shape[:dim], array.shape[dim + 1 :])
    return jnp.moveaxis(array.reshape(*before, length, -1, *after), dim, 0)


def summed_on_arrival(array, axis, dim):
    length = lax.axis_size(axis)
    pieces = lax.all_to_all(in_blocks(array, dim, length), axis, 0, 0, tiled=True)
    return jnp.sum(pieces.astype(jnp.float32), axis=0)


def in_one_piece(arrays, axis, dim, along):
    both = jnp.concatenate(arrays, axis=along)
    whole, at, outs = (summed_on_arrival(both, axis, dim), 0, [])
    for a in arrays:
        outs.append(lax.slice_in_dim(whole, at, at + a.shape[along], axis=along))
        at += a.shape[along]
    return tuple(outs)


def page_owners(table, lengths, pool_pages, page_len):
    pages = jnp.arange(pool_pages, dtype=jnp.int32)
    matches = table[:, :, None] == pages[None, None, :]
    ownership = jnp.any(matches, axis=1)
    slot_index = jnp.arange(table.shape[1], dtype=jnp.int32)
    position = jnp.sum(jnp.where(matches, slot_index[None, :, None], 0), axis=(0, 1))
    owner_length = jnp.sum(jnp.where(ownership, lengths[:, None], 0), axis=0)
    live_count = jnp.clip(owner_length - position * page_len, 0, page_len)
    return (ownership, live_count)


def attend(query_block, fresh_block, pool_block, table_block, length_block):
    step_count, req_count, head_count, head_width = query_block.shape
    pool_pages, page_len, kv_heads, _ = pool_block.shape
    group_size = head_count // kv_heads
    score_scale = 1.0 / math.sqrt(head_width)
    ownership, live_count = page_owners(table_block, length_block, pool_pages, page_len)
    owned_f = ownership.astype(jnp.float32)
    grouped = query_block.reshape(step_count, req_count, kv_heads, group_size, head_width)
    page_query = jnp.einsum(
        "rp,srkgd->pskgd",
        ownership.astype(jnp.bfloat16),
        grouped,
        preferred_element_type=jnp.float32,
    ).astype(jnp.bfloat16)
    key_rows = pool_block[..., :head_width]
    value_rows = pool_block[..., head_width:]
    page_scores = (
        jnp.einsum("pskgd,ptkd->pskgt", page_query, key_rows, preferred_element_type=jnp.float32)
        * score_scale
    )
    in_page = jnp.arange(page_len)[None, :] < live_count[:, None]
    page_scores = jnp.where(in_page[:, None, None, None, :], page_scores, NEG)
    fresh_keys = fresh_block[..., :head_width]
    fresh_values = fresh_block[..., head_width:]
    fresh_scores = (
        jnp.einsum("srkgd,urkd->srkgu", grouped, fresh_keys, preferred_element_type=jnp.float32)
        * score_scale
    )
    causal = jnp.arange(step_count)[:, None] >= jnp.arange(step_count)[None, :]
    fresh_scores = jnp.where(causal[:, None, None, None, :], fresh_scores, NEG)
    page_best = jnp.max(page_scores, axis=4)
    row_best = jnp.max(jnp.where(ownership[:, :, None, None, None], page_best[None], NEG), axis=1)
    row_best = jnp.maximum(row_best, jnp.moveaxis(jnp.max(fresh_scores, axis=4), 0, 1))
    owner_best = jnp.einsum("rp,rskg->pskg", owned_f, row_best, precision=EXACT)
    page_probs = jnp.exp(page_scores - owner_best[..., None])
    page_sum = jnp.sum(page_probs, axis=4)
    page_acc = jnp.einsum(
        "pskgt,ptkd->pskgd",
        page_probs.astype(jnp.bfloat16),
        value_rows,
        preferred_element_type=jnp.float32,
    )
    denominator = jnp.einsum("rp,pskg->rskg", owned_f, page_sum, precision=EXACT)
    numerator = jnp.einsum("rp,pskgd->rskgd", owned_f, page_acc, precision=EXACT)
    fresh_probs = jnp.exp(fresh_scores - jnp.moveaxis(row_best, 1, 0)[..., None])
    denominator = denominator + jnp.moveaxis(jnp.sum(fresh_probs, axis=4), 0, 1)
    numerator = numerator + jnp.einsum(
        "srkgu,urkd->rskgd",
        fresh_probs.astype(jnp.bfloat16),
        fresh_values,
        preferred_element_type=jnp.float32,
    )
    attended = jnp.moveaxis(numerator / denominator[..., None], 1, 0)
    return attended.reshape(step_count, req_count, head_count * head_width).astype(jnp.bfloat16)


def dispatch_keys(expert_ids, expert_total, local_experts, dp_count, capacity):
    step_count = expert_ids.shape[0]
    catalog = jnp.arange(expert_total, dtype=jnp.int32)
    named_mask = jnp.any(expert_ids[..., None] == catalog, axis=2).astype(jnp.int32)
    earlier = jnp.cumsum(named_mask, axis=1) - named_mask
    slot_rank = jnp.take_along_axis(earlier, expert_ids, axis=2)
    owner_index = expert_ids // local_experts
    local_index = expert_ids % local_experts
    step_index = jnp.arange(step_count, dtype=jnp.int32)[:, None, None]
    return ((local_index * dp_count + owner_index) * step_count + step_index) * capacity + slot_rank


def body(
    queries,
    fresh_kv,
    kv_pool,
    page_table,
    context_lengths,
    residual,
    out_weight,
    norm_gain,
    expert_ids,
    route_weights,
    gate_up,
    down_proj,
):
    attended = attend(queries, fresh_kv, kv_pool, page_table, context_lengths)
    step_count, req_count, head_cols = attended.shape
    flat_attended = attended.reshape(step_count * req_count, head_cols)
    partial_out = jnp.dot(
        flat_attended,
        lax.all_gather(out_weight, "dp", axis=1, tiled=True),
        preferred_element_type=jnp.float32,
    )
    projected = summed_on_arrival(partial_out.astype(jnp.bfloat16), "expert", 1)
    quarter = projected.shape[1]
    stream = residual.astype(jnp.float32).reshape(step_count * req_count, quarter) + projected
    squares = lax.psum(jnp.sum(stream * stream, axis=1), "expert")
    model_width = quarter * lax.axis_size("expert")
    inverse = lax.rsqrt(squares / model_width + EPS)
    normed = (stream * inverse[:, None] * norm_gain[None, :]).astype(jnp.bfloat16)
    dp_count = lax.axis_size("dp")
    local_experts = gate_up.shape[0]
    expert_total = local_experts * dp_count
    top_count = expert_ids.shape[2]
    capacity = min(
        req_count, max(2, (5 * req_count * top_count + 2 * expert_total - 1) // (2 * expert_total))
    )
    slot_keys = dispatch_keys(expert_ids, expert_total, local_experts, dp_count, capacity)
    slot_total = local_experts * dp_count * step_count * capacity
    slot_ids = jnp.arange(slot_total, dtype=jnp.int32)
    chosen = slot_keys.reshape(step_count * req_count, top_count)[None] == slot_ids[:, None, None]
    selector = jnp.any(chosen, axis=2).astype(jnp.bfloat16)
    outgoing = jnp.dot(selector, normed, preferred_element_type=jnp.float32).astype(jnp.bfloat16)
    outgoing = outgoing.reshape(local_experts, dp_count, step_count * capacity, quarter)
    incoming = lax.all_to_all(outgoing, "dp", split_axis=1, concat_axis=1, tiled=True)
    expert_rows = incoming.reshape(local_experts, dp_count * step_count * capacity, quarter)
    gate_part = jnp.einsum(
        "jmd,jdh->jmh", expert_rows, gate_up[:, 0], preferred_element_type=jnp.float32
    )
    up_part = jnp.einsum(
        "jmd,jdh->jmh", expert_rows, gate_up[:, 1], preferred_element_type=jnp.float32
    )
    gate_share, up_share = in_one_piece(
        (gate_part.astype(jnp.bfloat16), up_part.astype(jnp.bfloat16)), "expert", 2, 0
    )
    active_share = (jax.nn.silu(gate_share) * up_share).astype(jnp.bfloat16)
    activated = lax.all_gather(active_share, "expert", axis=2, tiled=True)
    expert_out = jnp.einsum(
        "jmh,jhd->jmd", activated, down_proj, preferred_element_type=jnp.float32
    ).astype(jnp.bfloat16)
    expert_out = expert_out.reshape(local_experts, dp_count, step_count * capacity, quarter)
    returned = lax.all_to_all(expert_out, "dp", split_axis=1, concat_axis=1, tiled=True)
    returned = returned.reshape(slot_total, quarter)
    picked = returned[slot_keys].astype(jnp.float32)
    share = route_weights / jnp.sum(route_weights, axis=2, keepdims=True)
    mixture = jnp.sum(share[..., None] * picked, axis=2)
    return (stream.reshape(step_count, req_count, quarter) + mixture).astype(jnp.bfloat16)


def solution(mesh):
    return jax.shard_map(
        body,
        mesh=mesh,
        in_specs=(
            P(None, ("groups", "dp"), "expert", None),
            P(None, ("groups", "dp"), "expert", None),
            P(("groups", "dp"), None, "expert", None),
            P(("groups", "dp"), None),
            P(("groups", "dp")),
            P(None, ("groups", "dp"), "expert"),
            P("expert", "dp"),
            P("expert"),
            P(None, ("groups", "dp"), None),
            P(None, ("groups", "dp"), None),
            P("dp", None, "expert", None),
            P("dp", None, "expert"),
        ),
        out_specs=P(None, ("groups", "dp"), "expert"),
        check_vma=False,
    )
```

profile of v0, /device:TPU:34, one launch (start us, length us, event | category | flops | bytes accessed | tf_op | source)
XLA Modules:
  0.0 382.7 jit_solution(539590098517076246)
XLA Ops:
  6.6 0.7 all-gather.2.cloned.1.call-update
  7.3 1.0 copy.119
  8.3 1.2 fusion
  9.5 0.7 select_reduce_fusion.2
  10.3 1.5 select_reduce_fusion
  11.9 1.4 convolution_convert_fusion.1
  13.3 4.5 %fusion.12 = (f32[320,2,8]{2,1,0:T(2,128)S(1)}, f32[320,2,8,16]{3,2,1,0:T(8,128)}) fusion(pred[320,16]{1,0:T(8,128)(4,1)S(1)} %iota_compare_fusion.2, bf16[320,16,1,256]{3,1,0,2:T(8,128)(2,1)} %bitcast.199, bf16[320,2,8,128]{3,0,2,1:T(8,128)(2,1)S(1)} %convolution_convert_fusion.1), kind=kOutput, calls=%fused_computation.20 | convolution fusion | flops 21212160 | bytes 2974720 | tf_op jit(solution)/shard_map/pskgd,ptkd->pskgt/dot_general | solution.py:61
  17.8 0.8 copy.123
  18.5 0.9 select_reduce_fusion.1
  20.0 1.9 fusion.86
  22.5 0.7 convolution_bitcast_fusion
  23.3 0.9 copy.127
  24.2 3.9 %fusion.10 = f32[320,2,8]{2,1,0:T(2,128)} fusion(f32[320,2,8,16]{3,2,1,0:T(8,128)} %get-tuple-element.12, f32[320,2,8]{2,1,0:T(2,128)S(1)} %copy.127, pred[320,16]{1,0:T(8,128)(4,1)S(1)} %iota_compare_fusion.2), kind=kLoop, calls=%fused_computation.18 | loop fusion | flops 322560 | bytes 373760 | tf_op jit(solution)/shard_map/reduce_sum | solution.py:79
  28.1 1.7 copy.132
  29.8 0.7 fusion.74
  30.6 0.8 fusion.63
  32.1 0.9 fusion.47
  32.9 1.0 fusion.66
  33.9 3.0 fusion.20
  37.0 1.6 fusion.42
  39.0 2.4 gather_fusion.1
  41.6 75.0 %all-gather.2.cloned.1.call-done = bf16[1024,4096]{1,0:T(8,128)(2,1)} async-done(((bf16[1024,128]{1,0:T(8,128)(2,1)}), bf16[1024,4096]{1,0:T(8,128)(2,1)}) %all-gather.2.cloned.1.call-update) | async-done | bytes 8388624 | tf_op jit(solution)/shard_map/all_gather | solution.py:131
  116.6 4.9 %convolution_convert_fusion = bf16[32,4096]{1,0:T(8,128)(2,1)S(1)} fusion(bf16[1024,4096]{1,0:T(8,128)(2,1)} %all-gather.2.cloned.1.call-done, bf16[4,8,8,128]{3,2,1,0:T(8,128)(2,1)S(1)} %bitcast.201), kind=kOutput, calls=%fused_computation.6 | convolution fusion | flops 268566528 | bytes 8716288 | tf_op jit(solution)/shard_map/dot_general | solution.py:129
  122.2 4.9 %all-to-all-start = ((bf16[4,32,1024]{2,1,0:T(8,128)(2,1)}), bf16[4,32,1024]{2,1,0:T(8,128)(2,1)S(1)}, u32[]{:S(2)}, u32[]{:S(2)}) async-start(bf16[4,32,1024]{2,1,0:T(8,128)(2,1)} %bitcast.198), calls=%async_computation | async-start | bytes 524288 | tf_op jit(solution)/shard_map/all_to_all | solution.py:20
  127.2 0.9 fusion.50
  128.1 4.7 %all-to-all-done = bf16[4,32,1024]{2,1,0:T(8,128)(2,1)S(1)} async-done(((bf16[4,32,1024]{2,1,0:T(8,128)(2,1)}), bf16[4,32,1024]{2,1,0:T(8,128)(2,1)S(1)}, u32[]{:S(2)}, u32[]{:S(2)}) %all-to-all-start) | async-done | bytes 262176 | tf_op jit(solution)/shard_map/all_to_all | solution.py:20
  132.8 0.9 multiply_reduce_fusion
  133.8 9.4 %psum.7 = f32[32]{0:T(128)S(1)} all-reduce(f32[32]{0:T(128)S(1)} %reduce_sum.96), channel_id=1, replica_groups=mesh['groups'=2,'dp'=32,'expert'=4] {'expert'}, use_global_device_ids=true, to_apply=%region_14.15 | all-reduce | flops 32 | bytes 256 | tf_op jit(solution)/shard_map/psum | solution.py:137
  143.2 0.9 fusion.54
  144.2 2.3 convolution_convert_fusion.3
  146.5 3.6 reshape.165
  150.1 3.1 copy.146
  153.2 74.8 %all_to_all.20 = bf16[2,32,10,1024]{3,0,2,1:T(2,128)(2,1)S(1)} all-to-all(bf16[2,32,10,1024]{3,0,2,1:T(2,128)(2,1)S(1)} %copy.146), channel_id=1, replica_groups=mesh['groups'=2,'dp'=32,'expert'=4] {'dp'}, dimensions={1} | all-to-all | bytes 2621440 | tf_op jit(solution)/shard_map/all_to_all | solution.py:155
  228.0 3.2 fusion.13
  231.3 1.2 fusion.16
  232.5 1.4 pad_maximum_fusion
  233.9 4.1 %copy.151 = bf16[4,320,768]{1,2,0:T(8,128)(2,1)} copy(bf16[4,320,768]{2,1,0:T(8,128)(2,1)} %pad_maximum_fusion) | data formatting | bytes 3932160 | tf_op jit(solution)/shard_map/concatenate | solution.py:25
  238.1 1.9 copy.152
  240.0 31.9 %all_to_all.21 = bf16[4,4,320,192]{2,3,1,0:T(8,128)(2,1)S(1)} all-to-all(bf16[4,4,320,192]{2,3,1,0:T(8,128)(2,1)S(1)} %copy.152), channel_id=1, replica_groups=mesh['groups'=2,'dp'=32,'expert'=4] {'expert'}, dimensions={0} | all-to-all | bytes 3932160 | tf_op jit(solution)/shard_map/all_to_all | solution.py:20
  272.4 14.5 %all_gather.7 = bf16[2,320,768]{1,2,0:T(8,128)(2,1)S(1)} all-gather(bf16[2,320,192]{1,2,0:T(8,128)(2,1)S(1)} %fusion.51), channel_id=1, replica_groups=mesh['groups'=2,'dp'=32,'expert'=4] {'expert'}, dimensions={2}, use_global_device_ids=true | all-gather | bytes 1228800 | tf_op jit(solution)/shard_map/all_gather | solution.py:167
  286.9 1.2 convolution_convert_fusion.2
  288.2 2.4 copy.153
  290.6 5.7 %all-to-all-start.3 = ((bf16[2,32,10,1024]{3,0,2,1:T(2,128)(2,1)}), bf16[2,32,10,1024]{3,0,2,1:T(2,128)(2,1)}, u32[]{:S(2)}, u32[]{:S(2)}) async-start(bf16[2,32,10,1024]{3,0,2,1:T(2,128)(2,1)} %bitcast.193), calls=%async_computation.3 | async-start | bytes 2621440 | tf_op jit(solution)/shard_map/all_to_all | solution.py:172
  296.5 66.6 %all-to-all-done.3 = bf16[2,32,10,1024]{3,0,2,1:T(2,128)(2,1)} async-done(((bf16[2,32,10,1024]{3,0,2,1:T(2,128)(2,1)}), bf16[2,32,10,1024]{3,0,2,1:T(2,128)(2,1)}, u32[]{:S(2)}, u32[]{:S(2)}) %all-to-all-start.3) | async-done | bytes 1310752 | tf_op jit(solution)/shard_map/all_to_all | solution.py:172
  363.1 3.2 copy.154
  366.3 3.6 reshape.169
  369.9 3.9 %gather_fusion = bf16[256,1024]{1,0:T(8,128)(2,1)} fusion(bf16[640,1024]{1,0:T(8,128)(2,1)} %reshape.169, s32[1024]{0:T(1024)S(1)} %pad_clamp_fusion), kind=kCustom, calls=%fused_computation | custom fusion | bytes 1049600 | tf_op jit(solution)/shard_map/gather | solution.py:174
  373.8 1.4 fusion.49
  (47 shorter events, 4.9 us)
Async XLA Ops:
  6.5 280.3 %copy-start = (bf16[2,768,1024]{2,1,0:T(8,128)(2,1)S(1)}, bf16[2,768,1024]{2,1,0:T(8,128)(2,1)}, u32[]{:S(2)}) copy-start(bf16[2,768,1024]{2,1,0:T(8,128)(2,1)} %param.23) | copy-start | bytes 9437188
  6.6 110.0 %all-gather.2.cloned.1.call-start = ((), (), s32[]{:S(2)}) async-start(), calls=%async_computation.4 | async-start | bytes 8650752 | tf_op jit(solution)/shard_map/all_gather | solution.py:131
  13.3 6.1 %copy-start.4 = (bf16[2,16,1,256]{3,1,2,0:T(8,128)(2,1)S(1)}, bf16[2,16,1,256]{3,1,2,0:T(8,128)(2,1)}, u32[]{:S(2)}) copy-start(bf16[2,16,1,256]{3,1,2,0:T(8,128)(2,1)} %param.13) | copy-start | bytes 49156
  21.9 0.6 copy-start.2
  37.0 1.7 copy-start.5
  122.2 10.6 %all-to-all-start = ((bf16[4,32,1024]{2,1,0:T(8,128)(2,1)}), bf16[4,32,1024]{2,1,0:T(8,128)(2,1)S(1)}, u32[]{:S(2)}, u32[]{:S(2)}) async-start(bf16[4,32,1024]{2,1,0:T(8,128)(2,1)} %bitcast.198), calls=%async_computation | async-start | bytes 524288 | tf_op jit(solution)/shard_map/all_to_all | solution.py:20
  150.1 81.2 %slice-start = ((s8[6291456]{0:T(1024)(128)(4,1)}), s8[2097152]{0:T(1024)(128)(4,1)S(1)}, s32[]{:S(2)}) async-start(s8[6291456]{0:T(1024)(128)(4,1)} %bitcast.203), calls=%async_computation.5 | async-start | bytes 4194304
  228.0 3.2 slice-start.1
  288.1 8.2 %copy-start.3 = (f32[2,16,8]{1,2,0:T(8,128)S(1)}, f32[2,16,8]{1,2,0:T(8,128)}, u32[]{:S(2)}) copy-start(f32[2,16,8]{1,2,0:T(8,128)} %param.21) | copy-start | bytes 3076
  290.6 72.6 %all-to-all-start.3 = ((bf16[2,32,10,1024]{3,0,2,1:T(2,128)(2,1)}), bf16[2,32,10,1024]{3,0,2,1:T(2,128)(2,1)}, u32[]{:S(2)}, u32[]{:S(2)}) async-start(bf16[2,32,10,1024]{3,0,2,1:T(2,128)(2,1)} %bitcast.193), calls=%async_computation.3 | async-start | bytes 2621440 | tf_op jit(solution)/shard_map/all_to_all | solution.py:172
  369.9 5.3 %copy-start.1 = (bf16[2,16,1024]{2,1,0:T(8,128)(2,1)S(1)}, bf16[2,16,1024]{2,1,0:T(8,128)(2,1)}, u32[]{:S(2)}) copy-start(bf16[2,16,1024]{2,1,0:T(8,128)(2,1)} %param.17) | copy-start | bytes 196612
Sparse Core Ops, SparseCore 0:
  9.1 107.4 all-gather.1
where the time goes:
time: 387 us; the launch traced here: 383 us
  waiting for transfers between devices  147 us (38%)
  blocking collectives  131 us (34%)
  local copies, waits for them, and re-layouts  35.8 us (9%)
  matrix products  27.9 us (7%)
  other arithmetic  17 us (4%)
  between operations  13.7 us (4%)
  starting transfers between devices  10.7 us (3%)
    all_gather x1, waiting for transfers between devices, body(): lax.all_gather(out_weight, 'dp', axis=1, tiled=True)  75 us
    all_to_all x1, blocking collectives, body(): lax.all_to_all(outgoing, 'dp', split_axis=1, concat_axis=1, tiled=True)  74.8 us
    all_to_all x1, waiting for transfers between devices, body(): lax.all_to_all(expert_out, 'dp', split_axis=1, concat_axis=1, tiled=True)  66.6 us
    all_to_all x1, blocking collectives, summed_on_arrival(): lax.all_to_all(in_blocks(array, dim, length), axis, 0, 0, tiled=True)  31.9 us
    all_gather x1, blocking collectives, body(): activated = lax.all_gather(active_share, 'expert', axis=2, tiled=True)  14.5 us
    psum x1, blocking collectives, body(): squares = lax.psum(jnp.sum(stream * stream, axis=1), 'expert')  9.37 us
  transfers between devices with their start and end apart: 3, of which 3 were waited for; matrix products, arithmetic and copies ran while one was open for 9% of the time, Pallas kernels for 0%

commit v1 on v0

--- a/solution.py
+++ b/solution.py
@@ -1,13 +1,17 @@
+import functools
 import math
 
 import jax
 import jax.numpy as jnp
 from jax import lax
+from jax.experimental import pallas as pl
+from jax.experimental.pallas import tpu as pltpu
 from jax.sharding import PartitionSpec as P
 
 NEG = -1e30
 EPS = 1e-06
 EXACT = lax.Precision.HIGHEST
+MESH = pl.DeviceIdType.MESH
 
 
 def in_blocks(array, dim, length):
@@ -19,15 +23,6 @@
     length = lax.axis_size(axis)
     pieces = lax.all_to_all(in_blocks(array, dim, length), axis, 0, 0, tiled=True)
     return jnp.sum(pieces.astype(jnp.float32), axis=0)
-
-
-def in_one_piece(arrays, axis, dim, along):
-    both = jnp.concatenate(arrays, axis=along)
-    whole, at, outs = (summed_on_arrival(both, axis, dim), 0, [])
-    for a in arrays:
-        outs.append(lax.slice_in_dim(whole, at, at + a.shape[along], axis=along))
-        at += a.shape[along]
-    return tuple(outs)
 
 
 def page_owners(table, lengths, pool_pages, page_len):
@@ -97,16 +92,423 @@
     return attended.reshape(step_count, req_count, head_count * head_width).astype(jnp.bfloat16)
 
 
-def dispatch_keys(expert_ids, expert_total, local_experts, dp_count, capacity):
-    step_count = expert_ids.shape[0]
+def rcopy(src, dst, send_sem, recv_sem, axis, target):
+    return pltpu.make_async_remote_copy(
+        src_ref=src,
+        dst_ref=dst,
+        send_sem=send_sem,
+        recv_sem=recv_sem,
+        device_id={axis: target},
+        device_id_type=MESH,
+    )
+
+
+def expert_kernel(
+    n_dp,
+    n_x,
+    slots,
+    block_ref,
+    gate_up_hbm,
+    down_hbm,
+    out_ref,
+    gath,
+    gate_up,
+    down,
+    mix_t,
+    rank_t,
+    pick,
+    slot_share,
+    part,
+    own,
+    in_opp,
+    in_left,
+    in_right,
+    act,
+    contrib,
+    mate_in,
+    sum_r,
+    sum_l,
+    ring_r,
+    ring_l,
+    w_sem,
+    ag_rs,
+    ag_rr,
+    ag_ls,
+    ag_lr,
+    ag_ms,
+    ag_mr,
+    x_s,
+    x_r,
+    a_s,
+    a_r,
+    m_s,
+    m_r,
+    rs_rs,
+    rs_rr,
+    rs_ls,
+    rs_lr,
+):
+    width = out_ref.shape[1]
+    hidden = act.shape[3]
+    locals_ = gate_up.shape[0]
+    rows = block_ref.shape[0]
+    half = rows // 2
+    chips = n_dp // 2
+    steps_r, steps_l = chips // 2, chips - 1 - chips // 2
+    chunk_dp = n_dp // n_x
+    chunk_rows = chunk_dp * rows
+    d = lax.axis_index("dp")
+    q = lax.axis_index("expert")
+    z, c = d // 2, d % 2
+    right, left, mate = (d + 2) % n_dp, (d + n_dp - 2) % n_dp, d + 1 - 2 * c
+    xr, xl, xo = (q + 1) % n_x, (q + n_x - 1) % n_x, (q + 2) % n_x
+
+    barrier = pltpu.get_barrier_semaphore()
+    for axis, target in (("dp", right), ("dp", left), ("dp", mate), ("expert", xr), ("expert", xl)):
+        pl.semaphore_signal(barrier, inc=1, device_id={axis: target}, device_id_type=MESH)
+
+    weights = [
+        pltpu.make_async_copy(gate_up_hbm, gate_up, w_sem.at[0]),
+        pltpu.make_async_copy(down_hbm, down, w_sem.at[1]),
+    ]
+    for w in weights:
+        w.start()
+    gath[d] = block_ref[...]
+    pl.semaphore_wait(barrier, 5)
+
+    def piece(ref, h):
+        return ref.at[pl.ds(h * half, half)]
+
+    def hop(idx, s, h, to_right):
+        send, recv, target = (ag_rs, ag_rr, right) if to_right else (ag_ls, ag_lr, left)
+        view = piece(gath.at[idx], h)
+        return rcopy(view, view, send.at[s, h], recv.at[s, h], "dp", target)
+
+    def to_mate(idx, k, h):
+        view = piece(gath.at[idx], h)
+        return rcopy(view, view, ag_ms.at[k, h], ag_mr.at[k, h], "dp", mate)
+
+    def first(h, send, recv, axis, target):
+        return rcopy(piece(block_ref, h), piece(gath.at[d], h), send, recv, axis, target)
+
+    firsts = []
+    for h in range(2):
+        firsts.append(first(h, ag_rs.at[0, h], ag_rr.at[0, h], "dp", right))
+        firsts.append(first(h, ag_ls.at[0, h], ag_lr.at[0, h], "dp", left))
+        firsts.append(first(h, ag_ms.at[0, h], ag_mr.at[0, h], "dp", mate))
+    for f in firsts:
+        f.start()
+
+    def from_left(s):
+        return (d + n_dp - 2 * s) % n_dp
+
+    def from_right(s):
+        return (d + 2 * s) % n_dp
+
+    def ag_step(s, carry):
+        for h in range(2):
+            hop(from_left(s), s - 1, h, True).wait_recv()
+            hop(from_left(s), s, h, True).start()
+            to_mate(from_left(s), s, h).start()
+            hop(from_right(s), s - 1, h, False).wait_recv()
+
+            @pl.when(s < steps_l)
+            def _():
+                hop(from_right(s), s, h, False).start()
+
+            to_mate(from_right(s), steps_r + s, h).start()
+        return carry
+
+    lax.fori_loop(1, steps_r, ag_step, 0)
+    for h in range(2):
+        hop(from_left(steps_r), steps_r - 1, h, True).wait_recv()
+        to_mate(from_left(steps_r), steps_r, h).start()
+
+    def ag_drain(k, carry):
+        for h in range(2):
+            to_mate(d, k, h).wait()
+
+            @pl.when(k < steps_r)
+            def _():
+                hop(d, k, h, True).wait_send()
+
+            @pl.when(k < steps_l)
+            def _():
+                hop(d, k, h, False).wait_send()
+
+        return carry
+
+    lax.fori_loop(0, chips, ag_drain, 0)
+    weights[0].wait()
+
+    t_row = lax.broadcasted_iota(jnp.int32, (chunk_rows, chunk_rows), 0)
+    t_col = lax.broadcasted_iota(jnp.int32, (chunk_rows, chunk_rows), 1)
+    below = jnp.where(t_row < t_col, 1.0, 0.0).astype(jnp.bfloat16)
+    slot_no = lax.broadcasted_iota(jnp.int32, (slots, chunk_rows), 0).astype(jnp.float32)
+    experts = n_dp * locals_
+
+    def project(r, keep):
+        both = gath[pl.ds(r * chunk_dp, chunk_dp)]
+        x = both[:, :, :width].reshape(chunk_rows, width)
+        mix = both[:, :, width:].reshape(chunk_rows, both.shape[2] - width)
+        mix_t[...] = jnp.transpose(mix.astype(jnp.float32))
+        named = jnp.where(mix_t[...] > 0.0, 1.0, 0.0).astype(jnp.bfloat16)
+        rank_t[...] = jnp.dot(named, below, preferred_element_type=jnp.float32)
+        for l in range(locals_):
+            e = d * locals_ + l
+            share = mix_t[pl.ds(e, 1), :] + mix_t[pl.ds(experts + e, 1), :]
+            hit = (rank_t[pl.ds(e, 1), :] == slot_no) & (share > 0.0)
+            chosen = jnp.where(hit, 1.0, 0.0)
+            at = pl.ds(l * slots, slots)
+            pick[r, at, :] = chosen.astype(jnp.bfloat16)
+            total = jnp.sum(chosen * share, axis=1, keepdims=True)
+            slot_share[r, at, :] = jnp.broadcast_to(total, (slots, slot_share.shape[2]))
+            picked = jnp.dot(
+                chosen.astype(jnp.bfloat16), x, preferred_element_type=jnp.float32
+            ).astype(jnp.bfloat16)
+            for g in range(2):
+                value = jnp.dot(picked, gate_up[l, g], preferred_element_type=jnp.float32)
+                keep(at, pl.ds(g * hidden, hidden), value)
+
+    def keep_part(r):
+        def keep(at, columns, value):
+            part[r, at, columns] = value.astype(jnp.bfloat16)
+
+        return keep
+
+    def keep_own(at, columns, value):
+        own[at, columns] = value
+
+    low, high = pl.ds(0, slots), pl.ds(slots, slots)
+
+    def xsend(src, dst, k, target):
+        return rcopy(src, dst, x_s.at[k], x_r.at[k], "expert", target)
+
+    opp_a = xsend(part.at[xo, low], in_opp.at[0], 0, xr)
+    opp_b = xsend(part.at[xo, high], in_opp.at[1], 1, xl)
+    right_b = xsend(part.at[xr, high], in_left.at[high], 2, xr)
+    left_a = xsend(part.at[xl, low], in_right.at[low], 3, xl)
+    right_a = xsend(part.at[xr, low], in_left.at[low], 4, xr)
+    left_b = xsend(part.at[xl, high], in_right.at[high], 5, xl)
+
+    project(xo, keep_part(xo))
+    opp_a.start()
+    opp_b.start()
+    project(xr, keep_part(xr))
+    right_b.start()
+    project(xl, keep_part(xl))
+    left_a.start()
+    project(q, keep_own)
+    opp_a.wait_recv()
+    part[xr, low, :] = (
+        part[xr, low, :].astype(jnp.float32) + in_opp[0].astype(jnp.float32)
+    ).astype(jnp.bfloat16)
+    right_a.start()
+    opp_b.wait_recv()
+    part[xl, high, :] = (
+        part[xl, high, :].astype(jnp.float32) + in_opp[1].astype(jnp.float32)
+    ).astype(jnp.bfloat16)
+    left_b.start()
+    right_b.wait_recv()
+    left_a.wait_recv()
+    right_a.wait_recv()
+    left_b.wait_recv()
+
+    def asend(owner, part_no, k, target):
+        view = act.at[owner, part_no]
+        return rcopy(view, view, a_s.at[k], a_r.at[k], "expert", target)
+
+    for l in range(2):
+        at = pl.ds(l * slots, slots)
+        total = own[at, :] + in_left[at, :].astype(jnp.float32) + in_right[at, :].astype(jnp.float32)
+        gate, up = total[:, :hidden], total[:, hidden:]
+        act[q, l] = (gate / (1.0 + jnp.exp(-gate)) * up).astype(jnp.bfloat16)
+        if l == 0:
+            asend(q, 0, 0, xr).start()
+        else:
+            asend(q, 1, 1, xl).start()
+    asend(q, 1, 2, xr).start()
+    asend(q, 0, 3, xl).start()
+    weights[1].wait()
+
+    def combine(r):
+        scaled = []
+        for l in range(locals_):
+            value = jnp.dot(act[r, l], down[l], preferred_element_type=jnp.float32)
+            scaled.append(value * slot_share[r, pl.ds(l * slots, slots), :1])
+        rows_out = jnp.concatenate(scaled, axis=0).astype(jnp.bfloat16)
+        mixed = lax.dot_general(
+            pick[r], rows_out, (((0,), (0,)), ((), ())), preferred_element_type=jnp.float32
+        ).astype(jnp.bfloat16)
+        for k in range(chunk_dp):
+            contrib[k % 2, r * (chunk_dp // 2) + k // 2] = mixed[k * rows : (k + 1) * rows]
+
+    def mate_send(r):
+        at = pl.ds(r * (chunk_dp // 2), chunk_dp // 2)
+        return rcopy(contrib.at[1 - c, at], mate_in.at[at], m_s.at[r], m_r.at[r], "dp", mate)
+
+    combine(q)
+    mate_send(q).start()
+    asend(xl, 0, 0, xr).wait_recv()
+    asend(xl, 0, 4, xr).start()
+    asend(xr, 1, 1, xl).wait_recv()
+    asend(xr, 1, 5, xl).start()
+    asend(xl, 1, 2, xr).wait_recv()
+    combine(xl)
+    mate_send(xl).start()
+    asend(xr, 0, 3, xl).wait_recv()
+    combine(xr)
+    mate_send(xr).start()
+    asend(xo, 0, 4, xr).wait_recv()
+    asend(xo, 1, 5, xl).wait_recv()
+    combine(xo)
+    mate_send(xo).start()
+    for r in (q, xl, xr, xo):
+        mate_send(r).wait_recv()
+
+    def ring(k, h, to_right):
+        if to_right:
+            return rcopy(
+                piece(sum_r.at[k], h), piece(ring_r.at[k], h), rs_rs.at[k, h], rs_rr.at[k, h], "dp", right
+            )
+        return rcopy(
+            piece(sum_l.at[k], h), piece(ring_l.at[k], h), rs_ls.at[k, h], rs_lr.at[k, h], "dp", left
+        )
+
+    def mine(chip, h):
+        at = pl.ds(h * half, half)
+        return contrib[c, chip, at].astype(jnp.float32) + mate_in[chip, at].astype(jnp.float32)
+
+    far_r = (z + steps_r) % chips
+    far_l = (z + chips - steps_l) % chips
+    for h in range(2):
+        at = pl.ds(h * half, half)
+        sum_r[0, at] = mine(far_r, h).astype(jnp.bfloat16)
+        ring(0, h, True).start()
+        sum_l[0, at] = mine(far_l, h).astype(jnp.bfloat16)
+        ring(0, h, False).start()
+
+    def rs_step(k, carry):
+        for h in range(2):
+            at = pl.ds(h * half, half)
+            ring(k - 1, h, True).wait_recv()
+            value = mine((z + steps_r - k) % chips, h) + ring_r[k - 1, at].astype(jnp.float32)
+            sum_r[k, at] = value.astype(jnp.bfloat16)
+            ring(k, h, True).start()
+
+            @pl.when(k < steps_l)
+            def _():
+                ring(k - 1, h, False).wait_recv()
+                other = mine((z + chips - steps_l + k) % chips, h) + ring_l[k - 1, at].astype(jnp.float32)
+                sum_l[k, at] = other.astype(jnp.bfloat16)
+                ring(k, h, False).start()
+
+        return carry
+
+    lax.fori_loop(1, steps_r, rs_step, 0)
+    for h in range(2):
+        at = pl.ds(h * half, half)
+        ring(steps_r - 1, h, True).wait_recv()
+        ring(steps_l - 1, h, False).wait_recv()
+        out_ref[at, :] = (
+            mine(z, h)
+            + ring_r[steps_r - 1, at].astype(jnp.float32)
+            + ring_l[steps_l - 1, at].astype(jnp.float32)
+        )
+
+    for copy in (opp_a, opp_b, right_b, left_a, right_a, left_b):
+        copy.wait_send()
+    asend(q, 0, 0, xr).wait_send()
+    asend(q, 1, 1, xl).wait_send()
+    asend(q, 1, 2, xr).wait_send()
+    asend(q, 0, 3, xl).wait_send()
+    asend(xl, 0, 4, xr).wait_send()
+    asend(xr, 1, 5, xl).wait_send()
+    for r in (q, xl, xr, xo):
+        mate_send(r).wait_send()
+
+    def rs_drain(k, carry):
+        for h in range(2):
+            ring(k, h, True).wait_send()
+
+            @pl.when(k < steps_l)
+            def _():
+                ring(k, h, False).wait_send()
+
+        return carry
+
+    lax.fori_loop(0, steps_r, rs_drain, 0)
+
+
+def expert_layer(block, gate_up, down_proj, per_step, steps):
+    n_dp, n_x = lax.axis_size("dp"), lax.axis_size("expert")
+    rows = block.shape[0]
+    locals_, _, width, hidden = gate_up.shape
+    chips = n_dp // 2
+    slots = (n_dp // n_x) * steps * per_step
+    chunk_rows = (n_dp // n_x) * rows
+    lanes = block.shape[1] - width
+    half_r, half_l = chips // 2, chips - 1 - chips // 2
+    bf16, f32, dma = jnp.bfloat16, jnp.float32, pltpu.SemaphoreType.DMA
+    vmem = pl.BlockSpec(memory_space=pltpu.VMEM)
+    anywhere = pl.BlockSpec(memory_space=pl.ANY)
+    return pl.pallas_call(
+        functools.partial(expert_kernel, n_dp, n_x, slots),
+        out_shape=jax.ShapeDtypeStruct((rows, width), f32),
+        in_specs=[vmem, anywhere, anywhere],
+        out_specs=vmem,
+        scratch_shapes=[
+            pltpu.VMEM((n_dp, rows, width + lanes), bf16),
+            pltpu.VMEM(gate_up.shape, bf16),
+            pltpu.VMEM(down_proj.shape, bf16),
+            pltpu.VMEM((lanes, chunk_rows), f32),
+            pltpu.VMEM((lanes, chunk_rows), f32),
+            pltpu.VMEM((n_x, locals_ * slots, chunk_rows), bf16),
+            pltpu.VMEM((n_x, locals_ * slots, 128), f32),
+            pltpu.VMEM((n_x, 2 * slots, 2 * hidden), bf16),
+            pltpu.VMEM((2 * slots, 2 * hidden), f32),
+            pltpu.VMEM((2, slots, 2 * hidden), bf16),
+            pltpu.VMEM((2 * slots, 2 * hidden), bf16),
+            pltpu.VMEM((2 * slots, 2 * hidden), bf16),
+            pltpu.VMEM((n_x, 2, slots, hidden), bf16),
+            pltpu.VMEM((2, chips, rows, width), bf16),
+            pltpu.VMEM((chips, rows, width), bf16),
+            pltpu.VMEM((half_r, rows, width), bf16),
+            pltpu.VMEM((half_l, rows, width), bf16),
+            pltpu.VMEM((half_r, rows, width), bf16),
+            pltpu.VMEM((half_l, rows, width), bf16),
+            dma((2,)),
+            dma((half_r, 2)),
+            dma((half_r, 2)),
+            dma((half_l, 2)),
+            dma((half_l, 2)),
+            dma((chips, 2)),
+            dma((chips, 2)),
+            dma((6,)),
+            dma((6,)),
+            dma((6,)),
+            dma((6,)),
+            dma((n_x,)),
+            dma((n_x,)),
+            dma((half_r, 2)),
+            dma((half_r, 2)),
+            dma((half_l, 2)),
+            dma((half_l, 2)),
+        ],
+        compiler_params=pltpu.CompilerParams(
+            collective_id=0, has_side_effects=True, vmem_limit_bytes=56 * 1024 * 1024
+        ),
+    )(block, gate_up, down_proj)
+
+
+def mix_columns(expert_ids, route_weights, expert_total):
+    share = route_weights / jnp.sum(route_weights, axis=2, keepdims=True)
     catalog = jnp.arange(expert_total, dtype=jnp.int32)
-    named_mask = jnp.any(expert_ids[..., None] == catalog, axis=2).astype(jnp.int32)
-    earlier = jnp.cumsum(named_mask, axis=1) - named_mask
-    slot_rank = jnp.take_along_axis(earlier, expert_ids, axis=2)
-    owner_index = expert_ids // local_experts
-    local_index = expert_ids % local_experts
-    step_index = jnp.arange(step_count, dtype=jnp.int32)[:, None, None]
-    return ((local_index * dp_count + owner_index) * step_count + step_index) * capacity + slot_rank
+    dense = jnp.sum(jnp.where(expert_ids[..., None] == catalog, share[..., None], 0.0), axis=2)
+    dense = dense.reshape(-1, expert_total)
+    top = dense.astype(jnp.bfloat16)
+    rest = (dense - top.astype(jnp.float32)).astype(jnp.bfloat16)
+    return jnp.concatenate([top, rest], axis=1)
 
 
 def body(
@@ -145,36 +547,9 @@
     capacity = min(
         req_count, max(2, (5 * req_count * top_count + 2 * expert_total - 1) // (2 * expert_total))
     )
-    slot_keys = dispatch_keys(expert_ids, expert_total, local_experts, dp_count, capacity)
-    slot_total = local_experts * dp_count * step_count * capacity
-    slot_ids = jnp.arange(slot_total, dtype=jnp.int32)
-    chosen = slot_keys.reshape(step_count * req_count, top_count)[None] == slot_ids[:, None, None]
-    selector = jnp.any(chosen, axis=2).astype(jnp.bfloat16)
-    outgoing = jnp.dot(selector, normed, preferred_element_type=jnp.float32).astype(jnp.bfloat16)
-    outgoing = outgoing.reshape(local_experts, dp_count, step_count * capacity, quarter)
-    incoming = lax.all_to_all(outgoing, "dp", split_axis=1, concat_axis=1, tiled=True)
-    expert_rows = incoming.reshape(local_experts, dp_count * step_count * capacity, quarter)
-    gate_part = jnp.einsum(
-        "jmd,jdh->jmh", expert_rows, gate_up[:, 0], preferred_element_type=jnp.float32
-    )
-    up_part = jnp.einsum(
-        "jmd,jdh->jmh", expert_rows, gate_up[:, 1], preferred_element_type=jnp.float32
-    )
-    gate_share, up_share = in_one_piece(
-        (gate_part.astype(jnp.bfloat16), up_part.astype(jnp.bfloat16)), "expert", 2, 0
-    )
-    active_share = (jax.nn.silu(gate_share) * up_share).astype(jnp.bfloat16)
-    activated = lax.all_gather(active_share, "expert", axis=2, tiled=True)
-    expert_out = jnp.einsum(
-        "jmh,jhd->jmd", activated, down_proj, preferred_element_type=jnp.float32
-    ).astype(jnp.bfloat16)
-    expert_out = expert_out.reshape(local_experts, dp_count, step_count * capacity, quarter)
-    returned = lax.all_to_all(expert_out, "dp", split_axis=1, concat_axis=1, tiled=True)
-    returned = returned.reshape(slot_total, quarter)
-    picked = returned[slot_keys].astype(jnp.float32)
-    share = route_weights / jnp.sum(route_weights, axis=2, keepdims=True)
-    mixture = jnp.sum(share[..., None] * picked, axis=2)
-    return (stream.reshape(step_count, req_count, quarter) + mixture).astype(jnp.bfloat16)
+    block = jnp.concatenate([normed, mix_columns(expert_ids, route_weights, expert_total)], axis=1)
+    mixture = expert_layer(block, gate_up, down_proj, capacity, step_count)
+    return (stream + mixture).reshape(step_count, req_count, quarter).astype(jnp.bfloat16)
 
 
 def solution(mesh):

time: 387 us -> 243 us (0.63); the launches traced: 383 us -> 243 us
  blocking collectives: 131 us -> 9.37 us
  Pallas kernels: 0 us -> 91.5 us
  waiting for transfers between devices: 147 us -> 99.8 us
  local copies, waits for them, and re-layouts: 35.8 us -> 3.15 us
  matrix products: 27.9 us -> 13.2 us
  other arithmetic: 17 us -> 7.6 us
  starting transfers between devices: 10.7 us -> 4.82 us
    all_to_all x2 -> x0, blocking collectives: 107 us -> none  [the longest x1 74.8 us: body(): lax.all_to_all(outgoing, 'dp', split_axis=1, concat_axis=1, tiled=True)]
    pallas_call x0 -> x1, Pallas kernels: none -> 91.5 us  [expert_layer(): pl.pallas_call(functools.partial(expert_kernel, n_dp, n_x, slots), out_sh...]
    all_to_all x1 -> x0, waiting for transfers between devices: 66.6 us -> none  [body(): lax.all_to_all(expert_out, 'dp', split_axis=1, concat_axis=1, tiled=True)]
    all_gather x1, waiting for transfers between devices: 75 us -> 93.5 us  [body(): lax.all_gather(out_weight, 'dp', axis=1, tiled=True)]
    all_gather x1 -> x0, blocking collectives: 14.5 us -> none  [body(): activated = lax.all_gather(active_share, 'expert', axis=2, tiled=True)]
    reshape x3 -> x0, local copies, waits for them, and re-layouts: 10.3 us -> none  [the longest x2 6.68 us: body(): outgoing.reshape(local_experts, dp_count, step_count * capacity, quarter)]
    dot_general x4 -> x0, matrix products: 8.02 us -> none  [the longest x1 3.22 us: body(): jnp.einsum('jmd,jdh->jmh', expert_rows, gate_up[:, 0], preferred_element_...]
    gather x4 -> x0, local copies, waits for them, and re-layouts: 6.47 us -> none  [the longest x1 3.86 us: body(): picked = returned[slot_keys].astype(jnp.float32)]
  transfers between devices with their start and end apart: 3 -> 2, of which waited for: 3 -> 2; matrix products, arithmetic and copies ran while one was open for 9% -> 6% of each run, Pallas kernels for 0% -> 0%
where the time goes in v1:
time: 243 us
  waiting for transfers between devices  99.8 us (41%)
  Pallas kernels  91.5 us (38%)
  between operations  13.6 us (6%)
  matrix products  13.2 us (5%)
  blocking collectives  9.37 us (4%)
  other arithmetic  7.6 us (3%)
  starting transfers between devices  4.82 us (2%)
  local copies, waits for them, and re-layouts  3.15 us (1%)
    all_gather x1, waiting for transfers between devices, body(): lax.all_gather(out_weight, 'dp', axis=1, tiled=True)  93.5 us
    pallas_call x1, Pallas kernels, expert_layer(): pl.pallas_call(functools.partial(expert_kernel, n_dp, n_x, slots), out_sh...  91.5 us
    psum x1, blocking collectives, body(): squares = lax.psum(jnp.sum(stream * stream, axis=1), 'expert')  9.37 us
    all_to_all x1, waiting for transfers between devices, summed_on_arrival(): lax.all_to_all(in_blocks(array, dim, length), axis, 0, 0, tiled=True)  5.61 us
    dot_general x1, matrix products, body(): jnp.dot(flat_attended, lax.all_gather(out_weight, 'dp', axis=1, tiled=Tru...  4.95 us
  transfers between devices with their start and end apart: 2, of which 2 were waited for; matrix products, arithmetic and copies ran while one was open for 6% of the time, Pallas kernels for 0%

profile of v1, /device:TPU:34, one launch (start us, length us, event | category | flops | bytes accessed | tf_op | source)
XLA Modules:
  0.0 243.1 jit_solution(13049722016924691441)
XLA Ops:
  6.5 0.0 copy-start
  6.6 0.0 all-gather.2.cloned.1.call-start
  6.6 0.7 all-gather.2.cloned.1.call-update
  7.3 0.8 copy.67
  8.2 1.2 fusion
  9.3 0.7 select_reduce_fusion.3
  10.1 1.5 select_reduce_fusion
  11.6 0.1 iota_compare_fusion.1
  11.7 0.0 copy-done
  11.7 0.5 convolution_convert_fusion.1
  12.2 0.0 copy-start.3
  12.3 3.0 %fusion.6 = (f32[320,2,8]{2,1,0:T(2,128)S(1)}, f32[320,2,8,16]{3,2,1,0:T(8,128)S(1)}) fusion(pred[320,16]{1,0:T(8,128)(4,1)S(1)} %iota_compare_fusion.1, bf16[320,16,1,256]{3,1,0,2:T(8,128)(2,1)} %bitcast.165, bf16[320,2,8,128]{3,0,2,1:T(8,128)(2,1)S(1)} %convolution_convert_fusion.1), kind=kOutput, calls=%fused_computation.11 | convolution fusion | flops 21212160 | bytes 2974720 | tf_op jit(solution)/shard_map/pskgd,ptkd->pskgt/dot_general | solution.py:56
  15.2 0.1 copy.71
  15.4 0.1 select_reduce_fusion.1
  15.5 0.0 copy-done.3
  15.6 0.4 fusion.55
  16.0 0.1 copy.74
  16.1 0.1 convolution_bitcast_fusion
  16.2 0.2 copy.75
  16.4 1.9 fusion.4
  18.3 0.1 copy.80
  18.4 0.1 fusion.42
  18.5 0.1 copy.81
  18.6 0.1 fusion.33
  18.7 0.2 fusion.45
  18.9 2.2 fusion.8
  21.2 0.0 copy-start.2
  21.2 0.0 copy-start.4
  21.2 1.6 fusion.28
  22.9 0.0 copy-done.2
  22.9 0.1 copy.85
  23.0 0.0 copy-done.4
  23.0 0.1 copy.84
  23.0 0.2 select_reduce_fusion.2
  23.2 93.5 %all-gather.2.cloned.1.call-done = bf16[1024,4096]{1,0:T(8,128)(2,1)} async-done(((bf16[1024,128]{1,0:T(8,128)(2,1)}), bf16[1024,4096]{1,0:T(8,128)(2,1)}) %all-gather.2.cloned.1.call-update) | async-done | bytes 8388624 | tf_op jit(solution)/shard_map/all_gather | solution.py:533
  116.7 5.0 %convolution_convert_fusion = bf16[32,4096]{1,0:T(8,128)(2,1)S(1)} fusion(bf16[1024,4096]{1,0:T(8,128)(2,1)} %all-gather.2.cloned.1.call-done, bf16[4,8,8,128]{3,2,1,0:T(8,128)(2,1)S(1)} %bitcast.167), kind=kOutput, calls=%fused_computation.3 | convolution fusion | flops 268566528 | bytes 8716288 | tf_op jit(solution)/shard_map/dot_general | solution.py:531
  121.7 0.7 copy.129
  122.4 4.8 %all-to-all-start = ((bf16[4,32,1024]{2,1,0:T(8,128)(2,1)}), bf16[4,32,1024]{2,1,0:T(8,128)(2,1)S(1)}, u32[]{:S(2)}, u32[]{:S(2)}) async-start(bf16[4,32,1024]{2,1,0:T(8,128)(2,1)} %bitcast.162), calls=%async_computation | async-start | bytes 524288 | tf_op jit(solution)/shard_map/all_to_all | solution.py:24
  127.2 5.6 %all-to-all-done = bf16[4,32,1024]{2,1,0:T(8,128)(2,1)S(1)} async-done(((bf16[4,32,1024]{2,1,0:T(8,128)(2,1)}), bf16[4,32,1024]{2,1,0:T(8,128)(2,1)S(1)}, u32[]{:S(2)}, u32[]{:S(2)}) %all-to-all-start) | async-done | bytes 262176 | tf_op jit(solution)/shard_map/all_to_all | solution.py:24
  132.8 0.0 copy-done.1
  132.9 0.1 multiply_reduce_fusion
  133.0 0.1 reduce_sum.86
  133.0 9.4 %psum.7 = f32[32]{0:T(128)S(1)} all-reduce(f32[32]{0:T(128)S(1)} %reduce_sum.86), channel_id=1, replica_groups=mesh['groups'=2,'dp'=32,'expert'=4] {'expert'}, use_global_device_ids=true, to_apply=%region_10.11 | all-reduce | flops 32 | bytes 256 | tf_op jit(solution)/shard_map/psum | solution.py:539
  142.4 0.0 copy-done.5
  142.4 0.1 multiply_convert_fusion
  142.5 0.7 concatenate.3.block_ref
  143.2 91.5 %shard_map.118 = f32[32,1024]{1,0:T(8,128)} custom-call(bf16[32,1152]{1,0:T(8,128)(2,1)} %concatenate.3.block_ref, bf16[2,2,1024,768]{3,2,1,0:T(8,128)(2,1)} %gate_up_hbm.1, bf16[2,768,1024]{2,1,0:T(8,128)(2,1)} %down_hbm.1), custom_call_target="tpu_custom_call" | custom-call | tf_op jit(solution)/shard_map/pallas_call | solution.py:455
  234.7 1.6 add_convert_fusion
  (13 shorter events, 0.1 us)
Async XLA Ops:
  6.5 5.1 %copy-start = (bf16[2,16,8,128]{3,2,1,0:T(8,128)(2,1)S(1)}, bf16[2,16,8,128]{3,2,1,0:T(8,128)(2,1)}, u32[]{:S(2)}) copy-start(bf16[2,16,8,128]{3,2,1,0:T(8,128)(2,1)} %param.12) | copy-start | bytes 196612
  6.6 110.1 %all-gather.2.cloned.1.call-start = ((), (), s32[]{:S(2)}) async-start(), calls=%async_computation.1 | async-start | bytes 8650752 | tf_op jit(solution)/shard_map/all_gather | solution.py:533
  12.2 3.3 %copy-start.3 = (bf16[2,16,1,256]{3,1,2,0:T(8,128)(2,1)S(1)}, bf16[2,16,1,256]{3,1,2,0:T(8,128)(2,1)}, u32[]{:S(2)}) copy-start(bf16[2,16,1,256]{3,1,2,0:T(8,128)(2,1)} %param.13) | copy-start | bytes 49156
  21.2 1.7 copy-start.2
  21.2 1.8 copy-start.4
  116.7 16.2 %copy-start.1 = (bf16[2,16,1024]{2,1,0:T(8,128)(2,1)S(1)}, bf16[2,16,1024]{2,1,0:T(8,128)(2,1)}, u32[]{:S(2)}) copy-start(bf16[2,16,1024]{2,1,0:T(8,128)(2,1)} %param.17) | copy-start | bytes 196612
  116.7 25.7 %copy-start.5 = (f32[1024]{0:T(1024)S(1)}, f32[1024]{0:T(1024)}, u32[]{:S(2)}) copy-start(f32[1024]{0:T(1024)} %param.19) | copy-start | bytes 12292
  122.4 10.4 %all-to-all-start = ((bf16[4,32,1024]{2,1,0:T(8,128)(2,1)}), bf16[4,32,1024]{2,1,0:T(8,128)(2,1)S(1)}, u32[]{:S(2)}, u32[]{:S(2)}) async-start(bf16[4,32,1024]{2,1,0:T(8,128)(2,1)} %bitcast.162), calls=%async_computation | async-start | bytes 524288 | tf_op jit(solution)/shard_map/all_to_all | solution.py:24
Sparse Core Ops, SparseCore 0:
  9.1 107.5 all-gather.1

commit v2 on v1

--- a/solution.py
+++ b/solution.py
@@ -12,17 +12,6 @@
 EPS = 1e-06
 EXACT = lax.Precision.HIGHEST
 MESH = pl.DeviceIdType.MESH
-
-
-def in_blocks(array, dim, length):
-    before, after = (array.shape[:dim], array.shape[dim + 1 :])
-    return jnp.moveaxis(array.reshape(*before, length, -1, *after), dim, 0)
-
-
-def summed_on_arrival(array, axis, dim):
-    length = lax.axis_size(axis)
-    pieces = lax.all_to_all(in_blocks(array, dim, length), axis, 0, 0, tiled=True)
-    return jnp.sum(pieces.astype(jnp.float32), axis=0)
 
 
 def page_owners(table, lengths, pool_pages, page_len):
@@ -103,14 +92,24 @@
     )
 
 
-def expert_kernel(
+def layer_kernel(
     n_dp,
     n_x,
     slots,
-    block_ref,
+    attended_ref,
+    residual_ref,
+    gain_ref,
+    out_weight_ref,
     gate_up_hbm,
     down_hbm,
     out_ref,
+    heads,
+    product,
+    back,
+    heads_in,
+    squares,
+    stream,
+    own_rows,
     gath,
     gate_up,
     down,
@@ -131,12 +130,12 @@
     ring_r,
     ring_l,
     w_sem,
-    ag_rs,
-    ag_rr,
-    ag_ls,
-    ag_lr,
-    ag_ms,
-    ag_mr,
+    back_s,
+    back_r,
+    h_s,
+    h_r,
+    q_s,
+    q_r,
     x_s,
     x_r,
     a_s,
@@ -147,16 +146,18 @@
     rs_rr,
     rs_ls,
     rs_lr,
+    *gather_sems,
 ):
-    width = out_ref.shape[1]
+    rows, width = out_ref.shape
     hidden = act.shape[3]
     locals_ = gate_up.shape[0]
-    rows = block_ref.shape[0]
     half = rows // 2
     chips = n_dp // 2
     steps_r, steps_l = chips // 2, chips - 1 - chips // 2
     chunk_dp = n_dp // n_x
     chunk_rows = chunk_dp * rows
+    head_cols = out_weight_ref.shape[0]
+    columns = out_weight_ref.shape[1]
     d = lax.axis_index("dp")
     q = lax.axis_index("expert")
     z, c = d // 2, d % 2
@@ -164,7 +165,8 @@
     xr, xl, xo = (q + 1) % n_x, (q + n_x - 1) % n_x, (q + 2) % n_x
 
     barrier = pltpu.get_barrier_semaphore()
-    for axis, target in (("dp", right), ("dp", left), ("dp", mate), ("expert", xr), ("expert", xl)):
+    neighbours = (("dp", right), ("dp", left), ("dp", mate), ("expert", xr), ("expert", xl), ("expert", xo))
+    for axis, target in neighbours:
         pl.semaphore_signal(barrier, inc=1, device_id={axis: target}, device_id_type=MESH)
 
     weights = [
@@ -173,73 +175,129 @@
     ]
     for w in weights:
         w.start()
-    gath[d] = block_ref[...]
-    pl.semaphore_wait(barrier, 5)
+    pl.semaphore_wait(barrier, len(neighbours))
 
     def piece(ref, h):
         return ref.at[pl.ds(h * half, half)]
 
-    def hop(idx, s, h, to_right):
-        send, recv, target = (ag_rs, ag_rr, right) if to_right else (ag_ls, ag_lr, left)
-        view = piece(gath.at[idx], h)
-        return rcopy(view, view, send.at[s, h], recv.at[s, h], "dp", target)
-
-    def to_mate(idx, k, h):
-        view = piece(gath.at[idx], h)
-        return rcopy(view, view, ag_ms.at[k, h], ag_mr.at[k, h], "dp", mate)
-
-    def first(h, send, recv, axis, target):
-        return rcopy(piece(block_ref, h), piece(gath.at[d], h), send, recv, axis, target)
-
-    firsts = []
-    for h in range(2):
-        firsts.append(first(h, ag_rs.at[0, h], ag_rr.at[0, h], "dp", right))
-        firsts.append(first(h, ag_ls.at[0, h], ag_lr.at[0, h], "dp", left))
-        firsts.append(first(h, ag_ms.at[0, h], ag_mr.at[0, h], "dp", mate))
-    for f in firsts:
-        f.start()
-
     def from_left(s):
         return (d + n_dp - 2 * s) % n_dp
 
     def from_right(s):
         return (d + 2 * s) % n_dp
 
-    def ag_step(s, carry):
-        for h in range(2):
-            hop(from_left(s), s - 1, h, True).wait_recv()
-            hop(from_left(s), s, h, True).start()
-            to_mate(from_left(s), s, h).start()
-            hop(from_right(s), s - 1, h, False).wait_recv()
-
-            @pl.when(s < steps_l)
-            def _():
-                hop(from_right(s), s, h, False).start()
-
-            to_mate(from_right(s), steps_r + s, h).start()
+    def mate_left(s):
+        return (mate + n_dp - 2 * s) % n_dp
+
+    def mate_right(s):
+        return (mate + 2 * s) % n_dp
+
+    class Gather:
+        def __init__(self, source, buffer, sems):
+            self.source, self.buffer = source, buffer
+            self.rs, self.rr, self.ls, self.lr, self.ms, self.mr = sems
+
+        def hop(self, idx, s, h, to_right):
+            send, recv, target = (self.rs, self.rr, right) if to_right else (self.ls, self.lr, left)
+            view = piece(self.buffer.at[idx], h)
+            return rcopy(view, view, send.at[s, h], recv.at[s, h], "dp", target)
+
+        def to_mate(self, idx, k, h):
+            view = piece(self.buffer.at[idx], h)
+            return rcopy(view, view, self.ms.at[k, h], self.mr.at[k, h], "dp", mate)
+
+        def begin(self):
+            for h in range(2):
+                src, dst = piece(self.source, h), piece(self.buffer.at[d], h)
+                rcopy(src, dst, self.rs.at[0, h], self.rr.at[0, h], "dp", right).start()
+                rcopy(src, dst, self.ls.at[0, h], self.lr.at[0, h], "dp", left).start()
+                rcopy(src, dst, self.ms.at[0, h], self.mr.at[0, h], "dp", mate).start()
+            self.buffer[d] = self.source[...]
+
+        def step(self, s):
+            for h in range(2):
+                self.hop(from_left(s), s - 1, h, True).wait_recv()
+                self.hop(from_left(s), s, h, True).start()
+                self.to_mate(from_left(s), s, h).start()
+                self.hop(from_right(s), s - 1, h, False).wait_recv()
+
+                @pl.when(s < steps_l)
+                def _():
+                    self.hop(from_right(s), s, h, False).start()
+
+                self.to_mate(from_right(s), steps_r + s, h).start()
+
+        def last(self):
+            for h in range(2):
+                self.hop(from_left(steps_r), steps_r - 1, h, True).wait_recv()
+                self.to_mate(from_left(steps_r), steps_r, h).start()
+
+        def await_mate(self, k):
+            for h in range(2):
+                self.to_mate(d, k, h).wait_recv()
+
+        def drain(self):
+            def one(k, carry):
+                for h in range(2):
+                    self.to_mate(d, k, h).wait_send()
+
+                    @pl.when(k < steps_r)
+                    def _():
+                        self.hop(d, k, h, True).wait_send()
+
+                    @pl.when(k < steps_l)
+                    def _():
+                        self.hop(d, k, h, False).wait_send()
+
+                return carry
+
+            lax.fori_loop(0, chips, one, 0)
+
+    first = Gather(attended_ref, heads, gather_sems[:6])
+    second = Gather(own_rows, gath, gather_sems[6:])
+
+    def give_back(idx):
+        return rcopy(product.at[idx], back.at[d], back_s.at[idx], back_r.at[d], "dp", idx)
+
+    def multiply(blocks):
+        x = jnp.concatenate([heads[b][:, :head_cols] for b in blocks], axis=0)
+        y = jnp.dot(x, out_weight_ref[...], preferred_element_type=jnp.float32).astype(jnp.bfloat16)
+        for k, b in enumerate(blocks):
+            product[b] = y[k * rows : (k + 1) * rows]
+
+    first.begin()
+
+    def heads_step(s, carry):
+        first.step(s)
+        first.await_mate(s - 1)
+
+        @pl.when(s > 1)
+        def _():
+            first.await_mate(steps_r + s - 1)
+
+        multiply([from_left(s), from_right(s), mate_left(s - 1), mate_right(s - 1)])
+        give_back(from_left(s)).start()
+        give_back(from_right(s)).start()
+        give_back(mate_left(s - 1)).start()
+
+        @pl.when(s > 1)
+        def _():
+            give_back(mate_right(s - 1)).start()
+
         return carry
 
-    lax.fori_loop(1, steps_r, ag_step, 0)
-    for h in range(2):
-        hop(from_left(steps_r), steps_r - 1, h, True).wait_recv()
-        to_mate(from_left(steps_r), steps_r, h).start()
-
-    def ag_drain(k, carry):
-        for h in range(2):
-            to_mate(d, k, h).wait()
-
-            @pl.when(k < steps_r)
-            def _():
-                hop(d, k, h, True).wait_send()
-
-            @pl.when(k < steps_l)
-            def _():
-                hop(d, k, h, False).wait_send()
-
-        return carry
-
-    lax.fori_loop(0, chips, ag_drain, 0)
-    weights[0].wait()
+    lax.fori_loop(1, steps_r, heads_step, 0)
+    first.last()
+    first.await_mate(steps_l)
+    first.await_mate(steps_r + steps_l)
+    multiply([from_left(steps_r), mate_left(steps_l), mate_right(steps_l), d])
+    give_back(from_left(steps_r)).start()
+    give_back(mate_left(steps_l)).start()
+    give_back(mate_right(steps_l)).start()
+    back[d] = product[d]
+    first.await_mate(steps_r)
+    multiply([mate_left(steps_r)])
+    give_back(mate_left(steps_r)).start()
 
     t_row = lax.broadcasted_iota(jnp.int32, (chunk_rows, chunk_rows), 0)
     t_col = lax.broadcasted_iota(jnp.int32, (chunk_rows, chunk_rows), 1)
@@ -247,10 +305,9 @@
     slot_no = lax.broadcasted_iota(jnp.int32, (slots, chunk_rows), 0).astype(jnp.float32)
     experts = n_dp * locals_
 
-    def project(r, keep):
-        both = gath[pl.ds(r * chunk_dp, chunk_dp)]
-        x = both[:, :, :width].reshape(chunk_rows, width)
-        mix = both[:, :, width:].reshape(chunk_rows, both.shape[2] - width)
+    def prepare(r, carry):
+        both = heads[pl.ds(r * chunk_dp, chunk_dp)]
+        mix = both[:, :, head_cols:].reshape(chunk_rows, heads.shape[2] - head_cols)
         mix_t[...] = jnp.transpose(mix.astype(jnp.float32))
         named = jnp.where(mix_t[...] > 0.0, 1.0, 0.0).astype(jnp.bfloat16)
         rank_t[...] = jnp.dot(named, below, preferred_element_type=jnp.float32)
@@ -263,9 +320,67 @@
             pick[r, at, :] = chosen.astype(jnp.bfloat16)
             total = jnp.sum(chosen * share, axis=1, keepdims=True)
             slot_share[r, at, :] = jnp.broadcast_to(total, (slots, slot_share.shape[2]))
-            picked = jnp.dot(
-                chosen.astype(jnp.bfloat16), x, preferred_element_type=jnp.float32
-            ).astype(jnp.bfloat16)
+        return carry
+
+    lax.fori_loop(0, n_x, prepare, 0)
+
+    def await_back(o, carry):
+        j = (d + o) % n_dp
+        rcopy(product.at[j], back.at[j], back_s.at[j], back_r.at[j], "dp", j).wait_recv()
+        return carry
+
+    lax.fori_loop(1, n_dp, await_back, 0)
+
+    def heads_send(k, target):
+        src = back.at[pl.ds(target * chunk_dp, chunk_dp)]
+        return rcopy(src, heads_in.at[k], h_s.at[k], h_r.at[k], "expert", target)
+
+    def squares_send(k, target):
+        return rcopy(squares.at[0], squares.at[k + 1], q_s.at[k], q_r.at[k], "expert", target)
+
+    peers = (xo, xr, xl)
+    for k, target in enumerate(peers):
+        heads_send(k, target).start()
+    for k, target in enumerate(peers):
+        heads_send(k, target).wait_recv()
+    square = jnp.zeros((rows, 1), jnp.float32)
+    for k in range(chunk_dp):
+        at = pl.ds(k * columns, columns)
+        value = residual_ref[:, at].astype(jnp.float32) + back[q * chunk_dp + k].astype(jnp.float32)
+        for p in range(len(peers)):
+            value = value + heads_in[p, k].astype(jnp.float32)
+        stream[:, at] = value
+        square = square + jnp.sum(value * value, axis=1, keepdims=True)
+    squares[0] = jnp.broadcast_to(square, squares.shape[1:])
+    for k, target in enumerate(peers):
+        squares_send(k, target).start()
+    for k, target in enumerate(peers):
+        squares_send(k, target).wait_recv()
+    whole = squares[0] + squares[1] + squares[2] + squares[3]
+    inverse = lax.rsqrt(whole[:, :1] / (width * n_x) + EPS)
+    own_rows[...] = (stream[...] * inverse * gain_ref[...]).astype(jnp.bfloat16)
+
+    second.begin()
+
+    def rows_step(s, carry):
+        second.step(s)
+        return carry
+
+    lax.fori_loop(1, steps_r, rows_step, 0)
+    second.last()
+
+    def rows_mate(k, carry):
+        second.await_mate(k)
+        return carry
+
+    lax.fori_loop(0, chips, rows_mate, 0)
+    weights[0].wait()
+
+    def project(r, keep):
+        x = gath[pl.ds(r * chunk_dp, chunk_dp)].reshape(chunk_rows, width)
+        for l in range(locals_):
+            at = pl.ds(l * slots, slots)
+            picked = jnp.dot(pick[r, at, :], x, preferred_element_type=jnp.float32).astype(jnp.bfloat16)
             for g in range(2):
                 value = jnp.dot(picked, gate_up[l, g], preferred_element_type=jnp.float32)
                 keep(at, pl.ds(g * hidden, hidden), value)
@@ -411,11 +526,23 @@
         ring(steps_r - 1, h, True).wait_recv()
         ring(steps_l - 1, h, False).wait_recv()
         out_ref[at, :] = (
-            mine(z, h)
+            stream[at, :]
+            + mine(z, h)
             + ring_r[steps_r - 1, at].astype(jnp.float32)
             + ring_l[steps_l - 1, at].astype(jnp.float32)
         )
 
+    first.drain()
+    second.drain()
+    for k, target in enumerate(peers):
+        heads_send(k, target).wait_send()
+        squares_send(k, target).wait_send()
+
+    def back_drain(o, carry):
+        give_back((d + o) % n_dp).wait_send()
+        return carry
+
+    lax.fori_loop(1, n_dp, back_drain, 0)
     for copy in (opp_a, opp_b, right_b, left_a, right_a, left_b):
         copy.wait_send()
     asend(q, 0, 0, xr).wait_send()
@@ -440,25 +567,35 @@
     lax.fori_loop(0, steps_r, rs_drain, 0)
 
 
-def expert_layer(block, gate_up, down_proj, per_step, steps):
+def layer(attended, residual, gain, out_weight, gate_up, down_proj, per_step, steps):
     n_dp, n_x = lax.axis_size("dp"), lax.axis_size("expert")
-    rows = block.shape[0]
+    rows = attended.shape[0]
     locals_, _, width, hidden = gate_up.shape
+    head_cols, columns = out_weight.shape
     chips = n_dp // 2
-    slots = (n_dp // n_x) * steps * per_step
-    chunk_rows = (n_dp // n_x) * rows
-    lanes = block.shape[1] - width
+    chunk_dp = n_dp // n_x
+    slots = chunk_dp * steps * per_step
+    chunk_rows = chunk_dp * rows
+    lanes = attended.shape[1] - head_cols
     half_r, half_l = chips // 2, chips - 1 - chips // 2
     bf16, f32, dma = jnp.bfloat16, jnp.float32, pltpu.SemaphoreType.DMA
     vmem = pl.BlockSpec(memory_space=pltpu.VMEM)
     anywhere = pl.BlockSpec(memory_space=pl.ANY)
+    gather_sems = [dma((n, 2)) for n in (half_r, half_r, half_l, half_l, chips, chips)]
     return pl.pallas_call(
-        functools.partial(expert_kernel, n_dp, n_x, slots),
+        functools.partial(layer_kernel, n_dp, n_x, slots),
         out_shape=jax.ShapeDtypeStruct((rows, width), f32),
-        in_specs=[vmem, anywhere, anywhere],
+        in_specs=[vmem, vmem, vmem, vmem, anywhere, anywhere],
         out_specs=vmem,
         scratch_shapes=[
-            pltpu.VMEM((n_dp, rows, width + lanes), bf16),
+            pltpu.VMEM((n_dp, rows, head_cols + lanes), bf16),
+            pltpu.VMEM((n_dp, rows, columns), bf16),
+            pltpu.VMEM((n_dp, rows, columns), bf16),
+            pltpu.VMEM((3, chunk_dp, rows, columns), bf16),
+            pltpu.VMEM((4, rows, 128), f32),
+            pltpu.VMEM((rows, width), f32),
+            pltpu.VMEM((rows, width), bf16),
+            pltpu.VMEM((n_dp, rows, width), bf16),
             pltpu.VMEM(gate_up.shape, bf16),
             pltpu.VMEM(down_proj.shape, bf16),
             pltpu.VMEM((lanes, chunk_rows), f32),
@@ -478,12 +615,12 @@
             pltpu.VMEM((half_r, rows, width), bf16),
             pltpu.VMEM((half_l, rows, width), bf16),
             dma((2,)),
-            dma((half_r, 2)),
-            dma((half_r, 2)),
-            dma((half_l, 2)),
-            dma((half_l, 2)),
-            dma((chips, 2)),
-            dma((chips, 2)),
+            dma((n_dp,)),
+            dma((n_dp,)),
+            dma((3,)),
+            dma((3,)),
+            dma((3,)),
+            dma((3,)),
             dma((6,)),
             dma((6,)),
             dma((6,)),
@@ -494,11 +631,13 @@
             dma((half_r, 2)),
             dma((half_l, 2)),
             dma((half_l, 2)),
+            *gather_sems,
+            *gather_sems,
         ],
         compiler_params=pltpu.CompilerParams(
             collective_id=0, has_side_effects=True, vmem_limit_bytes=56 * 1024 * 1024
         ),
-    )(block, gate_up, down_proj)
+    )(attended, residual, gain, out_weight, gate_up, down_proj)
 
 
 def mix_columns(expert_ids, route_weights, expert_total):
@@ -528,18 +667,6 @@
     attended = attend(queries, fresh_kv, kv_pool, page_table, context_lengths)
     step_count, req_count, head_cols = attended.shape
     flat_attended = attended.reshape(step_count * req_count, head_cols)
-    partial_out = jnp.dot(
-        flat_attended,
-        lax.all_gather(out_weight, "dp", axis=1, tiled=True),
-        preferred_element_type=jnp.float32,
-    )
-    projected = summed_on_arrival(partial_out.astype(jnp.bfloat16), "expert", 1)
-    quarter = projected.shape[1]
-    stream = residual.astype(jnp.float32).reshape(step_count * req_count, quarter) + projected
-    squares = lax.psum(jnp.sum(stream * stream, axis=1), "expert")
-    model_width = quarter * lax.axis_size("expert")
-    inverse = lax.rsqrt(squares / model_width + EPS)
-    normed = (stream * inverse[:, None] * norm_gain[None, :]).astype(jnp.bfloat16)
     dp_count = lax.axis_size("dp")
     local_experts = gate_up.shape[0]
     expert_total = local_experts * dp_count
@@ -547,9 +674,21 @@
     capacity = min(
         req_count, max(2, (5 * req_count * top_count + 2 * expert_total - 1) // (2 * expert_total))
     )
-    block = jnp.concatenate([normed, mix_columns(expert_ids, route_weights, expert_total)], axis=1)
-    mixture = expert_layer(block, gate_up, down_proj, capacity, step_count)
-    return (stream + mixture).reshape(step_count, req_count, quarter).astype(jnp.bfloat16)
+    quarter = residual.shape[2]
+    block = jnp.concatenate(
+        [flat_attended, mix_columns(expert_ids, route_weights, expert_total)], axis=1
+    )
+    out = layer(
+        block,
+        residual.reshape(step_count * req_count, quarter),
+        norm_gain[None, :],
+        out_weight,
+        gate_up,
+        down_proj,
+        capacity,
+        step_count,
+    )
+    return out.reshape(step_count, req_count, quarter).astype(jnp.bfloat16)
 
 
 def solution(mesh):

time: 243 us -> 181 us (0.74); the launches traced: 243 us -> 178 us
  waiting for transfers between devices: 99.8 us -> 0 us
  Pallas kernels: 91.5 us -> 160 us
  between operations: 13.6 us -> 0.22 us
  blocking collectives: 9.37 us -> 0 us
  matrix products: 13.2 us -> 8.28 us
  starting transfers between devices: 4.82 us -> 0 us
    all_gather x1 -> x0, waiting for transfers between devices: 93.5 us -> none  [body(): lax.all_gather(out_weight, 'dp', axis=1, tiled=True)]
    pallas_call x1, Pallas kernels: 91.5 us -> 160 us  [layer(): pl.pallas_call(functools.partial(layer_kernel, n_dp, n_x, slots), out_sha...]
    psum x1 -> x0, blocking collectives: 9.37 us -> none  [body(): squares = lax.psum(jnp.sum(stream * stream, axis=1), 'expert')]
    all_to_all x1 -> x0, waiting for transfers between devices: 5.61 us -> none  [summed_on_arrival(): lax.all_to_all(in_blocks(array, dim, length), axis, 0, 0, tiled=True)]
    dot_general x1 -> x0, matrix products: 4.95 us -> none  [body(): jnp.dot(flat_attended, lax.all_gather(out_weight, 'dp', axis=1, tiled=Tru...]
    all_to_all x1 -> x0, starting transfers between devices: 4.82 us -> none  [summed_on_arrival(): lax.all_to_all(in_blocks(array, dim, length), axis, 0, 0, tiled=True)]
  transfers between devices with their start and end apart: 2 -> 0, of which waited for: 2 -> 0; matrix products, arithmetic and copies ran while one was open for 6% -> 0% of each run, Pallas kernels for 0% -> 0%
where the time goes in v2:
time: 181 us; the launch traced here: 178 us
  Pallas kernels  160 us (88%)
  matrix products  8.28 us (5%)
  other arithmetic  7.36 us (4%)
  local copies, waits for them, and re-layouts  2.38 us (1%)
    pallas_call x1, Pallas kernels, layer(): pl.pallas_call(functools.partial(layer_kernel, n_dp, n_x, slots), out_sha...  160 us

profile of v2, /device:TPU:34, one launch (start us, length us, event | category | flops | bytes accessed | tf_op | source)
XLA Modules:
  0.0 178.1 jit_solution(9064899246922396857)
XLA Ops:
  0.0 0.0 copy-start
  0.0 0.9 copy.52
  0.9 1.2 fusion
  2.1 0.7 select_reduce_fusion.3
  2.8 1.5 select_reduce_fusion
  4.3 0.1 iota_compare_fusion.1
  4.4 0.0 copy-done
  4.4 0.5 convolution_convert_fusion
  5.0 0.0 copy-start.2
  5.0 3.0 %fusion.6 = (f32[320,2,8]{2,1,0:T(2,128)S(1)}, f32[320,2,8,16]{3,2,1,0:T(8,128)S(1)}) fusion(pred[320,16]{1,0:T(8,128)(4,1)S(1)} %iota_compare_fusion.1, bf16[320,16,1,256]{3,1,0,2:T(8,128)(2,1)} %bitcast.150, bf16[320,2,8,128]{3,0,2,1:T(8,128)(2,1)S(1)} %convolution_convert_fusion), kind=kOutput, calls=%fused_computation.10 | convolution fusion | flops 21212160 | bytes 2974720 | tf_op jit(solution)/shard_map/pskgd,ptkd->pskgt/dot_general | solution.py:45
  8.0 0.1 copy.56
  8.1 0.2 select_reduce_fusion.1
  8.3 0.0 copy-done.2
  8.3 0.4 fusion.53
  8.7 0.1 copy.59
  8.8 0.1 convolution_bitcast_fusion
  8.9 0.2 copy.60
  9.1 1.9 %fusion.4 = f32[320,2,8]{2,1,0:T(2,128)S(1)} fusion(f32[320,2,8,16]{3,2,1,0:T(8,128)S(1)} %get-tuple-element.12, f32[320,2,8]{2,1,0:T(2,128)S(1)} %copy.60, pred[320,16]{1,0:T(8,128)(4,1)S(1)} %iota_compare_fusion.1), kind=kLoop, calls=%fused_computation.8 | loop fusion | flops 322560 | bytes 373760 | tf_op jit(solution)/shard_map/reduce_sum | solution.py:63
  11.0 0.1 copy.65
  11.2 0.1 fusion.40
  11.2 0.1 copy.66
  11.3 0.1 fusion.33
  11.5 2.2 %fusion.8 = f32[320,2,8,128]{3,2,1,0:T(8,128)S(1)} fusion(f32[320,2,8,16]{3,2,1,0:T(8,128)S(1)} %get-tuple-element.12, bf16[320,16,1,256]{3,1,0,2:T(8,128)(2,1)} %bitcast.151, f32[320,2,8]{2,1,0:T(2,128)S(1)} %copy.60, pred[320,16]{1,0:T(8,128)(4,1)S(1)} %iota_compare_fusion.1), kind=kOutput, calls=%fused_computation.13 | convolution fusion | flops 21299200 | bytes 4285440 | tf_op jit(solution)/shard_map/pskgt,ptkd->pskgd/dot_general | solution.py:64
  13.7 0.0 copy-start.1
  13.7 0.0 copy-start.3
  13.7 0.2 fusion.43
  13.9 1.7 fusion.28
  15.6 0.0 copy-done.1
  15.7 0.1 copy.69
  15.7 0.0 copy-done.3
  15.7 0.1 copy.68
  15.8 0.2 select_reduce_fusion.2
  16.0 0.7 concatenate.3.attended_ref
  16.7 159.8 %shard_map.118 = f32[32,1024]{1,0:T(8,128)} custom-call(bf16[32,1152]{1,0:T(8,128)(2,1)} %concatenate.3.attended_ref, bf16[32,1024]{1,0:T(8,128)(2,1)} %bitcast.154, f32[1,1024]{1,0:T(1,128)} %bitcast.155, bf16[1024,128]{1,0:T(8,128)(2,1)} %out_weight_ref.1, bf16[2,2,1024,768]{3,2,1,0:T(8,128)(2,1)} %gate_up_hbm.1, bf16[2,768,1024]{2,1,0:T(8,128)(2,1)} %down_hbm.1), custom_call_target="tpu_custom_call" | custom-call | tf_op jit(solution)/shard_map/pallas_call | solution.py:585
  176.5 1.5 convert_element_type.46
  (10 shorter events, 0.1 us)
Async XLA Ops:
  0.0 4.4 %copy-start = (bf16[2,16,8,128]{3,2,1,0:T(8,128)(2,1)S(1)}, bf16[2,16,8,128]{3,2,1,0:T(8,128)(2,1)}, u32[]{:S(2)}) copy-start(bf16[2,16,8,128]{3,2,1,0:T(8,128)(2,1)} %param.12) | copy-start | bytes 196612
  5.0 3.3 %copy-start.2 = (bf16[2,16,1,256]{3,1,2,0:T(8,128)(2,1)S(1)}, bf16[2,16,1,256]{3,1,2,0:T(8,128)(2,1)}, u32[]{:S(2)}) copy-start(bf16[2,16,1,256]{3,1,2,0:T(8,128)(2,1)} %param.13) | copy-start | bytes 49156
  13.7 2.0 %copy-start.1 = (f32[2,16,8]{1,2,0:T(8,128)S(1)}, f32[2,16,8]{1,2,0:T(8,128)}, u32[]{:S(2)}) copy-start(f32[2,16,8]{1,2,0:T(8,128)} %param.21) | copy-start | bytes 3076
  13.7 2.1 %copy-start.3 = (s32[2,16,8]{1,2,0:T(8,128)S(1)}, s32[2,16,8]{1,2,0:T(8,128)}, u32[]{:S(2)}) copy-start(s32[2,16,8]{1,2,0:T(8,128)} %param.20) | copy-start | bytes 3076
